TPU v7x, 32 devices: a whole 2x2x4 slice. The times are simulated.
32 devices in a mesh: dp: 16 (over z, y, core), mp: 2 (over x).
Axes of the slice: x: 2, y: 2, z: 4, core: 2. Of those that a mesh axis runs over, the one named last changes fastest.
Arguments:
- inputs: bfloat16 [65536, 1024], P(('dp', 'mp')), may hold values from -6 to 6
- rand_blocks: int32 [16, 16, 62, 3], P('dp', 'mp'), may hold values from 1 to 62
- ln1_gain: float32 [1024], replicated, may hold values from 0.1 to 1.9
- ln1_bias: float32 [1024], replicated, may hold values from -4 to 4
- w_qkv: bfloat16 [3, 1024, 1024], P(None, None, 'mp'), may hold values from -0.1875 to 0.1875
- w_out: bfloat16 [1024, 1024], P('mp'), may hold values from -1.5 to 1.5
- ln2_gain: float32 [1024], replicated, may hold values from 0.1 to 1.9
- ln2_bias: float32 [1024], replicated, may hold values from -4 to 4
- w_up: bfloat16 [1024, 4096], P(None, 'mp'), may hold values from -0.1875 to 0.1875
- b_up: float32 [4096], P('mp'), may hold values from -6 to 6
- w_down: bfloat16 [4096, 1024], P('mp'), may hold values from -0.09375 to 0.09375
- b_down: float32 [1024], replicated, may hold values from -6 to 6
- cotangent: bfloat16 [65536, 1024], P(('dp', 'mp')), may hold values from -6 to 6
Outputs:
- output: float32 [65536, 1024], P(('dp', 'mp'))
- input_grad: float32 [65536, 1024], P(('dp', 'mp'))
- d_ln1_gain: float32 [1024], replicated
- d_ln1_bias: float32 [1024], replicated
- d_w_qkv: float32 [3, 1024, 1024], P(None, None, 'mp')
- d_w_out: float32 [1024, 1024], P('mp')
- d_ln2_gain: float32 [1024], replicated
- d_ln2_bias: float32 [1024], replicated
- d_w_up: float32 [1024, 4096], P(None, 'mp')
- d_b_up: float32 [4096], P('mp')
- d_w_down: float32 [4096, 1024], P('mp')
- d_b_down: float32 [1024], replicated
Inputs may be any that keep to these rules, and one draw needn't show every extreme that they name: `rand_blocks`: a block may appear more than once in a list and may equal a window or global block.
All inputs are finite; a program needn't handle non-finite values.
Results may differ from a plain program's by a relative error of at most 0.02.
Values may be sent and summed in bfloat16 or wider, within the bound.
A program may use at most 320 MiB of HBM per device.

v0:
```python
from functools import partial

import jax
import jax.numpy as jnp
from jax import lax
from jax.sharding import PartitionSpec as P

BLOCK = 64


EPSILON = 1e-05
PLAIN = (((1,), (1,)), ((), ()))
ROWWISE = (((0,), (0,)), ((), ()))
HIGH = lax.Precision.HIGHEST


def norm_rows(values, scale_vec, offset):
    centered = values - jnp.mean(values, axis=-1, keepdims=True)
    inv_std = lax.rsqrt(jnp.mean(centered * centered, axis=-1, keepdims=True) + EPSILON)
    normed = centered * inv_std
    return (normed * scale_vec + offset, normed, inv_std)


def norm_back(normed, inv_std, scale_vec, gradient):
    scaled = gradient * scale_vec
    inner_term = (
        scaled
        - jnp.mean(scaled, axis=-1, keepdims=True)
        - normed * jnp.mean(scaled * normed, axis=-1, keepdims=True)
    )
    return (inv_std * inner_term, jnp.sum(gradient * normed, 0), jnp.sum(gradient, 0))


def gelu_tanh(values):
    return jax.nn.gelu(values, approximate=True)


def block_table(random_rows, num_blocks):
    rows_idx = jnp.arange(num_blocks, dtype=jnp.int32)[:, None]
    steps_off = jnp.arange(-1, 2, dtype=jnp.int32)[None, :]
    window = jnp.clip(rows_idx + steps_off, 0, num_blocks - 1)
    filler = jnp.zeros((1, random_rows.shape[1]), jnp.int32)
    chosen = jnp.concatenate([filler, random_rows, filler], 0)
    first_cols = jnp.zeros((num_blocks, 1), jnp.int32)
    last_cols = first_cols + (num_blocks - 1)
    return jnp.concatenate([first_cols, last_cols, window, chosen], 1)


def make_selector(table_grp, num_blocks):
    flat_table = table_grp.reshape(-1)
    return (flat_table[:, None] == jnp.arange(num_blocks, dtype=jnp.int32)[None, :]).astype(
        jnp.bfloat16
    )


def pick_blocks(selector, both_flat, per_query, block_rows, head_width):
    picked = jnp.dot(selector, both_flat, preferred_element_type=jnp.float32).astype(jnp.bfloat16)
    picked = picked.reshape(8, per_query, 2, block_rows, head_width)
    key_grp = picked[:, :, 0].reshape(8, per_query * block_rows, head_width)
    value_grp = picked[:, :, 1].reshape(8, per_query * block_rows, head_width)
    return (key_grp, value_grp)


def attend_item(operands):
    query, keys, values, table = operands
    num_blocks, per_query = table.shape
    seq_len, head_width = query.shape
    block_rows = seq_len // num_blocks
    scaling = head_width ** (-0.5)
    both_flat = jnp.stack(
        [
            keys.reshape(num_blocks, block_rows * head_width),
            values.reshape(num_blocks, block_rows * head_width),
        ],
        1,
    ).reshape(num_blocks, 2 * block_rows * head_width)
    query_groups = query.reshape(num_blocks // 8, 8, block_rows, head_width)
    table_groups = table.reshape(num_blocks // 8, 8, per_query)

    def group_scores(group_ops):
        query_grp, table_grp = group_ops
        selector = make_selector(table_grp, num_blocks)
        key_grp, value_grp = pick_blocks(selector, both_flat, per_query, block_rows, head_width)
        scores = (
            jnp.einsum("nqd,nkd->nqk", query_grp, key_grp, preferred_element_type=jnp.float32)
            * scaling
        )
        highest = jnp.max(scores, axis=-1, keepdims=True)
        shifted = jnp.exp(scores - highest)
        totals = jnp.sum(shifted, axis=-1, keepdims=True)
        weights_low = (shifted / totals).astype(jnp.bfloat16)
        mixed_grp = jnp.einsum(
            "nqk,nkd->nqd", weights_low, value_grp, preferred_element_type=jnp.float32
        )
        return (mixed_grp, (highest + jnp.log(totals))[..., 0])

    mixed, sparse_log = lax.map(group_scores, (query_groups, table_groups))
    mixed = mixed.reshape(seq_len, head_width)
    end_rows = jnp.concatenate([query[:block_rows], query[seq_len - block_rows :]], 0)
    glob_scores = (
        lax.dot_general(end_rows, keys, PLAIN, preferred_element_type=jnp.float32) * scaling
    )
    glob_high = jnp.max(glob_scores, axis=-1, keepdims=True)
    glob_exp = jnp.exp(glob_scores - glob_high)
    glob_total = jnp.sum(glob_exp, axis=-1, keepdims=True)
    glob_mixed = jnp.dot(
        (glob_exp / glob_total).astype(jnp.bfloat16), values, preferred_element_type=jnp.float32
    )
    mixed = mixed.at[:block_rows].set(glob_mixed[:block_rows])
    mixed = mixed.at[seq_len - block_rows :].set(glob_mixed[block_rows:])
    return (mixed.astype(jnp.bfloat16), sparse_log, (glob_high + jnp.log(glob_total))[:, 0])


def attend_back(operands):
    query, keys, values, table, out_grad, sparse_log, glob_log = operands
    num_blocks, per_query = table.shape
    seq_len, head_width = query.shape
    block_rows = seq_len // num_blocks
    scaling = head_width ** (-0.5)
    both_flat = jnp.stack(
        [
            keys.reshape(num_blocks, block_rows * head_width),
            values.reshape(num_blocks, block_rows * head_width),
        ],
        1,
    ).reshape(num_blocks, 2 * block_rows * head_width)
    query_groups = query.reshape(num_blocks // 8, 8, block_rows, head_width)
    table_groups = table.reshape(num_blocks // 8, 8, per_query)
    inner_blocks = jnp.arange(num_blocks) % (num_blocks - 1) != 0
    grad_blocks = out_grad.reshape(num_blocks, block_rows, head_width)
    grad_blocks = jnp.where(inner_blocks[:, None, None], grad_blocks, jnp.zeros_like(grad_blocks))
    grad_groups = grad_blocks.reshape(num_blocks // 8, 8, block_rows, head_width)

    def group_back(carry, group_ops):
        query_grp, table_grp, grad_grp, log_grp = group_ops
        selector = make_selector(table_grp, num_blocks)
        key_grp, value_grp = pick_blocks(selector, both_flat, per_query, block_rows, head_width)
        scores = (
            jnp.einsum("nqd,nkd->nqk", query_grp, key_grp, preferred_element_type=jnp.float32)
            * scaling
        )
        probs = jnp.exp(scores - log_grp[..., None])
        prob_grad = jnp.einsum(
            "nqd,nkd->nqk", grad_grp, value_grp, preferred_element_type=jnp.float32
        )
        inner_sum = jnp.sum(probs * prob_grad, axis=-1, keepdims=True)
        score_grad = (probs * (prob_grad - inner_sum)).astype(jnp.bfloat16)
        query_grad = (
            jnp.einsum("nqk,nkd->nqd", score_grad, key_grp, preferred_element_type=jnp.float32)
            * scaling
        )
        key_part = (
            jnp.einsum("nqk,nqd->nkd", score_grad, query_grp, preferred_element_type=jnp.float32)
            * scaling
        )
        value_part = jnp.einsum(
            "nqk,nqd->nkd", probs.astype(jnp.bfloat16), grad_grp, preferred_element_type=jnp.float32
        )
        parts = jnp.stack(
            [
                key_part.reshape(8 * per_query, block_rows * head_width),
                value_part.reshape(8 * per_query, block_rows * head_width),
            ],
            1,
        )
        parts = parts.reshape(8 * per_query, 2 * block_rows * head_width)
        carry = carry + lax.dot_general(
            selector.astype(jnp.float32),
            parts,
            ROWWISE,
            precision=HIGH,
            preferred_element_type=jnp.float32,
        )
        return (carry, query_grad)

    zero_blocks = jnp.zeros((num_blocks, 2 * block_rows * head_width), jnp.float32)
    accum, query_grad = lax.scan(
        group_back, zero_blocks, (query_groups, table_groups, grad_groups, sparse_log)
    )
    accum = accum.reshape(num_blocks, 2, block_rows, head_width)
    key_acc = accum[:, 0].reshape(seq_len, head_width)
    value_acc = accum[:, 1].reshape(seq_len, head_width)
    query_grad = query_grad.reshape(seq_len, head_width)
    end_rows = jnp.concatenate([query[:block_rows], query[seq_len - block_rows :]], 0)
    end_grad = jnp.concatenate([out_grad[:block_rows], out_grad[seq_len - block_rows :]], 0)
    glob_scores = (
        lax.dot_general(end_rows, keys, PLAIN, preferred_element_type=jnp.float32) * scaling
    )
    glob_probs = jnp.exp(glob_scores - glob_log[:, None])
    glob_pgrad = lax.dot_general(end_grad, values, PLAIN, preferred_element_type=jnp.float32)
    glob_inner = jnp.sum(glob_probs * glob_pgrad, axis=-1, keepdims=True)
    glob_sgrad = (glob_probs * (glob_pgrad - glob_inner)).astype(jnp.bfloat16)
    glob_qgrad = jnp.dot(glob_sgrad, keys, preferred_element_type=jnp.float32) * scaling
    query_grad = query_grad.at[:block_rows].add(glob_qgrad[:block_rows])
    query_grad = query_grad.at[seq_len - block_rows :].add(glob_qgrad[block_rows:])
    key_grad = (
        key_acc
        + lax.dot_general(glob_sgrad, end_rows, ROWWISE, preferred_element_type=jnp.float32)
        * scaling
    )
    value_grad = value_acc + lax.dot_general(
        glob_probs.astype(jnp.bfloat16), end_grad, ROWWISE, preferred_element_type=jnp.float32
    )
    return (query_grad, key_grad, value_grad)


def per_device(
    inputs,
    rand_blocks,
    ln1_gain,
    ln1_bias,
    w_qkv,
    w_out,
    ln2_gain,
    ln2_bias,
    w_up,
    b_up,
    w_down,
    b_down,
    cotangent,
):
    seqs_here = rand_blocks.shape[0]
    heads_here = rand_blocks.shape[1]
    item_count = seqs_here * heads_here
    head_width = w_qkv.shape[2] // heads_here
    residual_in = inputs.astype(jnp.float32)
    normed_one, normed_a, inv_a = norm_rows(residual_in, ln1_gain, ln1_bias)
    first_rows = lax.all_gather(normed_one.astype(jnp.bfloat16), "mp", axis=0, tiled=True)
    group_rows = first_rows.shape[0]
    seq_len = group_rows // seqs_here
    num_blocks = seq_len // BLOCK
    projected = jnp.einsum(
        "td,cde->cte", first_rows, w_qkv, preferred_element_type=jnp.float32
    ).astype(jnp.bfloat16)
    heads_qkv = projected.reshape(3, seqs_here, seq_len, heads_here, head_width).transpose(
        0, 1, 3, 2, 4
    )
    heads_qkv = heads_qkv.reshape(3, item_count, seq_len, head_width)
    tables = jax.vmap(partial(block_table, num_blocks=num_blocks))(
        rand_blocks.reshape(item_count, num_blocks - 2, rand_blocks.shape[3])
    )
    mixed, sparse_log, glob_log = lax.map(
        attend_item, (heads_qkv[0], heads_qkv[1], heads_qkv[2], tables)
    )
    attn_mix = (
        mixed.reshape(seqs_here, heads_here, seq_len, head_width)
        .transpose(0, 2, 1, 3)
        .reshape(group_rows, heads_here * head_width)
    )
    attn_out = lax.psum_scatter(
        jnp.dot(attn_mix, w_out, preferred_element_type=jnp.float32).astype(jnp.bfloat16),
        "mp",
        scatter_dimension=0,
        tiled=True,
    ).astype(jnp.float32)
    mid_resid = residual_in + attn_out
    normed_two, normed_b, inv_b = norm_rows(mid_resid, ln2_gain, ln2_bias)
    second_rows, grad_rows = (
        lax.all_gather(normed_two.astype(jnp.bfloat16), "mp", axis=0, tiled=True),
        lax.all_gather(cotangent, "mp", axis=0, tiled=True),
    )
    hidden_pre = jnp.dot(second_rows, w_up, preferred_element_type=jnp.float32) + b_up
    hidden_act = gelu_tanh(hidden_pre).astype(jnp.bfloat16)
    branch_out = lax.psum_scatter(
        jnp.dot(hidden_act, w_down, preferred_element_type=jnp.float32).astype(jnp.bfloat16),
        "mp",
        scatter_dimension=0,
        tiled=True,
    ).astype(jnp.float32)
    result = mid_resid + (branch_out + b_down)
    grad_own = cotangent.astype(jnp.float32)
    bias_down_grad = jnp.sum(grad_own, 0)
    down_grad = lax.dot_general(hidden_act, grad_rows, ROWWISE, preferred_element_type=jnp.float32)
    act_grad = lax.dot_general(grad_rows, w_down, PLAIN, preferred_element_type=jnp.float32)
    gelu_pull = jax.vjp(gelu_tanh, hidden_pre)[1]
    pre_grad = gelu_pull(act_grad)[0].astype(jnp.bfloat16)
    bias_up_grad = jnp.sum(pre_grad.astype(jnp.float32), 0)
    up_grad = lax.dot_general(second_rows, pre_grad, ROWWISE, preferred_element_type=jnp.float32)
    second_grad = lax.psum_scatter(
        lax.dot_general(pre_grad, w_up, PLAIN, preferred_element_type=jnp.float32).astype(
            jnp.bfloat16
        ),
        "mp",
        scatter_dimension=0,
        tiled=True,
    ).astype(jnp.float32)
    mid_part, gain_two_grad, bias_two_grad = norm_back(normed_b, inv_b, ln2_gain, second_grad)
    mid_grad = grad_own + mid_part
    attn_grad_rows = lax.all_gather(mid_grad.astype(jnp.bfloat16), "mp", axis=0, tiled=True)
    out_grad = lax.dot_general(
        attn_mix, attn_grad_rows, ROWWISE, preferred_element_type=jnp.float32
    )
    mix_grad = lax.dot_general(
        attn_grad_rows, w_out, PLAIN, preferred_element_type=jnp.float32
    ).astype(jnp.bfloat16)
    mix_items = (
        mix_grad.reshape(seqs_here, seq_len, heads_here, head_width)
        .transpose(0, 2, 1, 3)
        .reshape(item_count, seq_len, head_width)
    )
    query_grads, key_grads, value_grads = lax.map(
        attend_back,
        (heads_qkv[0], heads_qkv[1], heads_qkv[2], tables, mix_items, sparse_log, glob_log),
    )
    stacked = jnp.stack([query_grads, key_grads, value_grads]).astype(jnp.bfloat16)
    stacked = (
        stacked.reshape(3, seqs_here, heads_here, seq_len, head_width)
        .transpose(0, 1, 3, 2, 4)
        .reshape(3, group_rows, heads_here * head_width)
    )
    qkv_grad = jnp.einsum("td,cte->cde", first_rows, stacked, preferred_element_type=jnp.float32)
    first_grad = lax.psum_scatter(
        jnp.einsum("cte,cde->td", stacked, w_qkv, preferred_element_type=jnp.float32).astype(
            jnp.bfloat16
        ),
        "mp",
        scatter_dimension=0,
        tiled=True,
    ).astype(jnp.float32)
    input_part, gain_one_grad, bias_one_grad = norm_back(normed_a, inv_a, ln1_gain, first_grad)
    input_grad = mid_grad + input_part
    small_sums = lax.psum(
        (gain_one_grad, bias_one_grad, gain_two_grad, bias_two_grad, bias_down_grad), ("dp", "mp")
    )
    qkv_grad, out_grad, up_grad, bias_up_grad, down_grad = (
        lax.psum(qkv_grad.astype(jnp.bfloat16), "dp").astype(jnp.float32),
        lax.psum(out_grad.astype(jnp.bfloat16), "dp").astype(jnp.float32),
        lax.psum(up_grad.astype(jnp.bfloat16), "dp").astype(jnp.float32),
        lax.psum(bias_up_grad.astype(jnp.bfloat16), "dp").astype(jnp.float32),
        lax.psum(down_grad.astype(jnp.bfloat16), "dp").astype(jnp.float32),
    )
    return (
        result,
        input_grad,
        small_sums[0],
        small_sums[1],
        qkv_grad,
        out_grad,
        small_sums[2],
        small_sums[3],
        up_grad,
        bias_up_grad,
        down_grad,
        small_sums[4],
    )


def solution(mesh):
    return jax.shard_map(
        per_device,
        mesh=mesh,
        in_specs=(
            P(("dp", "mp"), None),
            P("dp", "mp", None, None),
            P(),
            P(),
            P(None, None, "mp"),
            P("mp", None),
            P(),
            P(),
            P(None, "mp"),
            P("mp"),
            P("mp", None),
            P(),
            P(("dp", "mp"), None),
        ),
        out_specs=(
            P(("dp", "mp"), None),
            P(("dp", "mp"), None),
            P(),
            P(),
            P(None, None, "mp"),
            P("mp", None),
            P(),
            P(),
            P(None, "mp"),
            P("mp"),
            P("mp", None),
            P(),
        ),
        check_vma=False,
    )
```

profile of v0, /device:TPU:0, one launch (start us, length us, event | category | flops | bytes accessed | tf_op | source)
XLA Modules:
  0.0 5234.4 jit_solution(17163692770296250939)
XLA Ops:
  17.8 106.0 %all-gather.5.cloned.1.call-done = bf16[4096,1024]{1,0:T(8,128)(2,1)} async-done(((bf16[2048,1024]{1,0:T(8,128)(2,1)}), bf16[4096,1024]{1,0:T(8,128)(2,1)}) %all-gather.5.cloned.1.call-update) | async-done | bytes 8388624 | tf_op jit(solution)/shard_map/all_gather | solution.py:228
  182.6 964.2 %while.96 = (s32[]{:T(128)}, bf16[8,4096,64]{1,2,0:T(8,128)(2,1)}, f32[8,8,8,64]{3,2,1,0:T(8,128)}, f32[8,128]{1,0:T(8,128)}, bf16[8,4096,64]{2,1,0:T(8,128)(2,1...) while((s32[]{:T(128)}, bf16[8,4096,64]{1,2,0:T(8,128)(2,1)}, ...), condition=%wide.region_9.10_spmd, body=%wide.region_2.9_spmd.sunk | while | flops 275025280 | bytes 29968956 | solution.py:242
  200.6 93.5 %while.99 = (s32[]{:T(128)}, bf16[8,8,64,64]{3,2,1,0:T(8,128)(2,1)}, f32[8,8,64]{2,1,0:T(8,128)S(1)}, bf16[8,8,64,64]{3,2,1,0:T(8,128)(2,1)}, s32[8,8,8]{2,1,0:T...) while((s32[]{:T(128)}, bf16[8,8,64,64]{3,2,1,0:T(8,128)(2,1)}, f32[8,8,64]{2,1,0:T(8,128)S(1)}, ...), condition=%wide.region_6.6_spmd, body=%wide.region_3.5_spmd.sunk | while | flops 136580608 | bytes 10903893 | solution.py:97
  321.1 93.5 %while.99 = (s32[]{:T(128)}, bf16[8,8,64,64]{3,2,1,0:T(8,128)(2,1)}, f32[8,8,64]{2,1,0:T(8,128)S(1)}, bf16[8,8,64,64]{3,2,1,0:T(8,128)(2,1)}, s32[8,8,8]{2,1,0:T...) while((s32[]{:T(128)}, bf16[8,8,64,64]{3,2,1,0:T(8,128)(2,1)}, f32[8,8,64]{2,1,0:T(8,128)S(1)}, ...), condition=%wide.region_6.6_spmd, body=%wide.region_3.5_spmd.sunk | while | flops 136580608 | bytes 10903893 | solution.py:97
  441.6 93.5 %while.99 = (s32[]{:T(128)}, bf16[8,8,64,64]{3,2,1,0:T(8,128)(2,1)}, f32[8,8,64]{2,1,0:T(8,128)S(1)}, bf16[8,8,64,64]{3,2,1,0:T(8,128)(2,1)}, s32[8,8,8]{2,1,0:T...) while((s32[]{:T(128)}, bf16[8,8,64,64]{3,2,1,0:T(8,128)(2,1)}, f32[8,8,64]{2,1,0:T(8,128)S(1)}, ...), condition=%wide.region_6.6_spmd, body=%wide.region_3.5_spmd.sunk | while | flops 136580608 | bytes 10903893 | solution.py:97
  562.0 93.5 %while.99 = (s32[]{:T(128)}, bf16[8,8,64,64]{3,2,1,0:T(8,128)(2,1)}, f32[8,8,64]{2,1,0:T(8,128)S(1)}, bf16[8,8,64,64]{3,2,1,0:T(8,128)(2,1)}, s32[8,8,8]{2,1,0:T...) while((s32[]{:T(128)}, bf16[8,8,64,64]{3,2,1,0:T(8,128)(2,1)}, f32[8,8,64]{2,1,0:T(8,128)S(1)}, ...), condition=%wide.region_6.6_spmd, body=%wide.region_3.5_spmd.sunk | while | flops 136580608 | bytes 10903893 | solution.py:97
  682.5 93.5 %while.99 = (s32[]{:T(128)}, bf16[8,8,64,64]{3,2,1,0:T(8,128)(2,1)}, f32[8,8,64]{2,1,0:T(8,128)S(1)}, bf16[8,8,64,64]{3,2,1,0:T(8,128)(2,1)}, s32[8,8,8]{2,1,0:T...) while((s32[]{:T(128)}, bf16[8,8,64,64]{3,2,1,0:T(8,128)(2,1)}, f32[8,8,64]{2,1,0:T(8,128)S(1)}, ...), condition=%wide.region_6.6_spmd, body=%wide.region_3.5_spmd.sunk | while | flops 136580608 | bytes 10903893 | solution.py:97
  802.9 93.5 %while.99 = (s32[]{:T(128)}, bf16[8,8,64,64]{3,2,1,0:T(8,128)(2,1)}, f32[8,8,64]{2,1,0:T(8,128)S(1)}, bf16[8,8,64,64]{3,2,1,0:T(8,128)(2,1)}, s32[8,8,8]{2,1,0:T...) while((s32[]{:T(128)}, bf16[8,8,64,64]{3,2,1,0:T(8,128)(2,1)}, f32[8,8,64]{2,1,0:T(8,128)S(1)}, ...), condition=%wide.region_6.6_spmd, body=%wide.region_3.5_spmd.sunk | while | flops 136580608 | bytes 10903893 | solution.py:97
  923.4 93.5 %while.99 = (s32[]{:T(128)}, bf16[8,8,64,64]{3,2,1,0:T(8,128)(2,1)}, f32[8,8,64]{2,1,0:T(8,128)S(1)}, bf16[8,8,64,64]{3,2,1,0:T(8,128)(2,1)}, s32[8,8,8]{2,1,0:T...) while((s32[]{:T(128)}, bf16[8,8,64,64]{3,2,1,0:T(8,128)(2,1)}, f32[8,8,64]{2,1,0:T(8,128)S(1)}, ...), condition=%wide.region_6.6_spmd, body=%wide.region_3.5_spmd.sunk | while | flops 136580608 | bytes 10903893 | solution.py:97
  1043.8 93.5 %while.99 = (s32[]{:T(128)}, bf16[8,8,64,64]{3,2,1,0:T(8,128)(2,1)}, f32[8,8,64]{2,1,0:T(8,128)S(1)}, bf16[8,8,64,64]{3,2,1,0:T(8,128)(2,1)}, s32[8,8,8]{2,1,0:T...) while((s32[]{:T(128)}, bf16[8,8,64,64]{3,2,1,0:T(8,128)(2,1)}, f32[8,8,64]{2,1,0:T(8,128)S(1)}, ...), condition=%wide.region_6.6_spmd, body=%wide.region_3.5_spmd.sunk | while | flops 136580608 | bytes 10903893 | solution.py:97
  1157.5 99.4 %reduce-scatter.5.cloned.1.call-done = bf16[2048,1024]{1,0:T(8,128)(2,1)} async-done(((bf16[4096,1024]{1,0:T(8,128)(2,1)}), bf16[2048,1024]{1,0:T(8,128)(2,1)}) %reduce-scatter.5.cloned.1.call-update) | async-done | bytes 4194320 | tf_op jit(solution)/shard_map/reduce_scatter | solution.py:250
  1269.3 103.5 %all-gather.7.cloned.1.call-done = bf16[4096,1024]{1,0:T(8,128)(2,1)} async-done(((bf16[2048,1024]{1,0:T(8,128)(2,1)}), bf16[4096,1024]{1,0:T(8,128)(2,1)}) %all-gather.7.cloned.1.call-update) | async-done | bytes 8388624 | tf_op jit(solution)/shard_map/all_gather | solution.py:259
  1547.4 99.4 %reduce-scatter.9.cloned.1.call-done = bf16[2048,1024]{1,0:T(8,128)(2,1)} async-done(((bf16[4096,1024]{1,0:T(8,128)(2,1)}), bf16[2048,1024]{1,0:T(8,128)(2,1)}) %reduce-scatter.9.cloned.1.call-update) | async-done | bytes 4194320 | tf_op jit(solution)/shard_map/reduce_scatter | solution.py:279
  1786.3 2913.1 %while.98 = (s32[]{:T(128)}, bf16[8,4096,64]{1,2,0:T(8,128)(2,1)}, bf16[8,4096,64]{1,2,0:T(8,128)(2,1)}, bf16[8,4096,64]{1,2,0:T(8,128)(2,1)}, bf16[8,4096,64]{2...) while((s32[]{:T(128)}, bf16[8,4096,64]{1,2,0:T(8,128)(2,1)}, ...), condition=%wide.region_22.23_spmd, body=%wide.region_17.22_spmd.sunk | while | flops 983490496 | bytes 111270584 | solution.py:301
  1809.6 307.4 %while.100 = (s32[]{:T(128)}, f32[64,8192]{1,0:T(8,128)}, f32[8,8,64,64]{3,2,1,0:T(8,128)}, s32[8,8,8]{2,1,0:T(8,128)S(1)}, bf16[8,8,64,64]{3,2,1,0:T(8,128)(2,1...) while((s32[]{:T(128)}, f32[64,8192]{1,0:T(8,128)}, ...), condition=%wide.region_20.20_spmd.clone, body=%wide.region_18.19_spmd.clone.sunk | while | flops 642031104 | bytes 48511176 | solution.py:177
  2173.7 307.4 %while.100 = (s32[]{:T(128)}, f32[64,8192]{1,0:T(8,128)}, f32[8,8,64,64]{3,2,1,0:T(8,128)}, s32[8,8,8]{2,1,0:T(8,128)S(1)}, bf16[8,8,64,64]{3,2,1,0:T(8,128)(2,1...) while((s32[]{:T(128)}, f32[64,8192]{1,0:T(8,128)}, ...), condition=%wide.region_20.20_spmd.clone, body=%wide.region_18.19_spmd.clone.sunk | while | flops 642031104 | bytes 48511176 | solution.py:177
  2537.7 307.4 %while.100 = (s32[]{:T(128)}, f32[64,8192]{1,0:T(8,128)}, f32[8,8,64,64]{3,2,1,0:T(8,128)}, s32[8,8,8]{2,1,0:T(8,128)S(1)}, bf16[8,8,64,64]{3,2,1,0:T(8,128)(2,1...) while((s32[]{:T(128)}, f32[64,8192]{1,0:T(8,128)}, ...), condition=%wide.region_20.20_spmd.clone, body=%wide.region_18.19_spmd.clone.sunk | while | flops 642031104 | bytes 48511176 | solution.py:177
  2901.8 307.4 %while.100 = (s32[]{:T(128)}, f32[64,8192]{1,0:T(8,128)}, f32[8,8,64,64]{3,2,1,0:T(8,128)}, s32[8,8,8]{2,1,0:T(8,128)S(1)}, bf16[8,8,64,64]{3,2,1,0:T(8,128)(2,1...) while((s32[]{:T(128)}, f32[64,8192]{1,0:T(8,128)}, ...), condition=%wide.region_20.20_spmd.clone, body=%wide.region_18.19_spmd.clone.sunk | while | flops 642031104 | bytes 48511176 | solution.py:177
  3265.9 307.4 %while.100 = (s32[]{:T(128)}, f32[64,8192]{1,0:T(8,128)}, f32[8,8,64,64]{3,2,1,0:T(8,128)}, s32[8,8,8]{2,1,0:T(8,128)S(1)}, bf16[8,8,64,64]{3,2,1,0:T(8,128)(2,1...) while((s32[]{:T(128)}, f32[64,8192]{1,0:T(8,128)}, ...), condition=%wide.region_20.20_spmd.clone, body=%wide.region_18.19_spmd.clone.sunk | while | flops 642031104 | bytes 48511176 | solution.py:177
  3629.9 307.4 %while.100 = (s32[]{:T(128)}, f32[64,8192]{1,0:T(8,128)}, f32[8,8,64,64]{3,2,1,0:T(8,128)}, s32[8,8,8]{2,1,0:T(8,128)S(1)}, bf16[8,8,64,64]{3,2,1,0:T(8,128)(2,1...) while((s32[]{:T(128)}, f32[64,8192]{1,0:T(8,128)}, ...), condition=%wide.region_20.20_spmd.clone, body=%wide.region_18.19_spmd.clone.sunk | while | flops 642031104 | bytes 48511176 | solution.py:177
  3994.0 307.4 %while.100 = (s32[]{:T(128)}, f32[64,8192]{1,0:T(8,128)}, f32[8,8,64,64]{3,2,1,0:T(8,128)}, s32[8,8,8]{2,1,0:T(8,128)S(1)}, bf16[8,8,64,64]{3,2,1,0:T(8,128)(2,1...) while((s32[]{:T(128)}, f32[64,8192]{1,0:T(8,128)}, ...), condition=%wide.region_20.20_spmd.clone, body=%wide.region_18.19_spmd.clone.sunk | while | flops 642031104 | bytes 48511176 | solution.py:177
  4358.0 307.4 %while.100 = (s32[]{:T(128)}, f32[64,8192]{1,0:T(8,128)}, f32[8,8,64,64]{3,2,1,0:T(8,128)}, s32[8,8,8]{2,1,0:T(8,128)S(1)}, bf16[8,8,64,64]{3,2,1,0:T(8,128)(2,1...) while((s32[]{:T(128)}, f32[64,8192]{1,0:T(8,128)}, ...), condition=%wide.region_20.20_spmd.clone, body=%wide.region_18.19_spmd.clone.sunk | while | flops 642031104 | bytes 48511176 | solution.py:177
  4811.8 154.5 %all-reduce.4.cloned.1.call-done = (bf16[3,1024,512]{1,2,0:T(8,128)(2,1)}, bf16[512,1024]{1,0:T(8,128)(2,1)}, bf16[1024,2048]{1,0:T(8,128)(2,1)}, bf16[2048,1024]{1,0:T(8,128)(2,1)}) async-done(((bf16[3,1024,512]{1,2,0:T(8,128)(2,1)}, bf16[512,1024]{1,0:T(8,128)(2,1)}, bf16[1024,2048]{1,0:T(8,128)(2,1)}, bf16[2048,1024]{1,0:T(8,128)(2,1)}), (bf16[3,1024,512]{1,2,0:T(8,128)(2,1)}, ...) | async-done | bytes 12582928 | tf_op jit(solution)/shard_map/psum | solution.py:326
  5074.7 96.1 %reduce-scatter.7.cloned.1.call-done = bf16[2048,1024]{1,0:T(8,128)(2,1)} async-done(((bf16[4096,1024]{1,0:T(8,128)(2,1)}), bf16[2048,1024]{1,0:T(8,128)(2,1)}) %reduce-scatter.7.cloned.1.call-update) | async-done | bytes 4194320 | tf_op jit(solution)/shard_map/reduce_scatter | solution.py:264
  (2725 shorter events, 4553.5 us)
Async XLA Ops:
  7.2 116.7 %copy-start = (bf16[3,1024,512]{2,1,0:T(8,128)(2,1)S(1)}, bf16[3,1024,512]{2,1,0:T(8,128)(2,1)}, u32[]{:S(2)}) copy-start(bf16[3,1024,512]{2,1,0:T(8,128)(2,1)} %param.33) | copy-start | bytes 9437188
  7.2 116.6 %all-gather.5.cloned.1.call-start = ((), (), s32[]{:S(2)}) async-start(), calls=%async_computation.4 | async-start | bytes 12582912 | tf_op jit(solution)/shard_map/all_gather | solution.py:228
  17.0 1239.9 %reduce-scatter.5.cloned.1.call-start = ((), (), s32[]{:S(2)}) async-start(), calls=%async_computation.5 | async-start | bytes 12582912 | tf_op jit(solution)/shard_map/reduce_scatter | solution.py:250
  1157.4 107.8 %copy-start.30 = (f32[1024]{0:T(1024)S(1)}, f32[1024]{0:T(1024)}, u32[]{:S(2)}) copy-start(f32[1024]{0:T(1024)} %param.35) | copy-start | bytes 12292
  1157.4 107.8 %copy-start.39 = (f32[1024]{0:T(1024)S(1)}, f32[1024]{0:T(1024)}, u32[]{:S(2)}) copy-start(f32[1024]{0:T(1024)} %param.36) | copy-start | bytes 12292
  1157.4 215.4 %all-gather.7.cloned.1.call-start = ((), (), s32[]{:S(2)}) async-start(), calls=%async_computation.6 | async-start | bytes 12582912 | tf_op jit(solution)/shard_map/all_gather | solution.py:259
  1265.2 107.6 %copy-start.43 = (f32[2048]{0:T(1024)S(1)}, f32[2048]{0:T(1024)}, u32[]{:S(2)}) copy-start(f32[2048]{0:T(1024)} %param.38) | copy-start | bytes 24580
  1268.7 209.6 %all-gather.9.cloned.1.call-start = ((), (), s32[]{:S(2)}) async-start(), calls=%async_computation.8 | async-start | bytes 12582912 | tf_op jit(solution)/shard_map/all_gather | solution.py:260
  1269.3 377.5 %reduce-scatter.9.cloned.1.call-start = ((), (), s32[]{:S(2)}) async-start(), calls=%async_computation.9 | async-start | bytes 12582912 | tf_op jit(solution)/shard_map/reduce_scatter | solution.py:279
  1547.3 99.5 %copy-start.17 = (f32[2048]{0:T(1024)S(1)}, f32[2048]{0:T(1024)}, u32[]{:S(2)}) copy-start(f32[2048]{0:T(1024)} %copy-done.16) | copy-start | bytes 24580
  1547.3 99.5 %copy-start.22 = (f32[2048]{0:T(1024)S(1)}, f32[2048]{0:T(1024)}, u32[]{:S(2)}) copy-start(f32[2048]{0:T(1024)} %copy-done.21) | copy-start | bytes 24580
  1547.3 99.5 %copy-start.31 = (f32[1024]{0:T(1024)S(1)}, f32[1024]{0:T(1024)}, u32[]{:S(2)}) copy-start(f32[1024]{0:T(1024)} %param.35) | copy-start | bytes 12292
  1547.3 220.5 %all-gather.11.cloned.1.call-start = ((), (), s32[]{:S(2)}) async-start(), calls=%async_computation.10 | async-start | bytes 12582912 | tf_op jit(solution)/shard_map/all_gather | solution.py:289
  1663.7 3302.6 %all-reduce.4.cloned.1.call-start = ((), (), s32[]{:S(2)}) async-start(), calls=%async_computation.12 | async-start | bytes 25165824 | tf_op jit(solution)/shard_map/psum | solution.py:326
  4733.5 335.0 %reduce-scatter.11.cloned.1.call-start = ((), (), s32[]{:S(2)}) async-start(), calls=%async_computation.11 | async-start | bytes 12582912 | tf_op jit(solution)/shard_map/reduce_scatter | solution.py:312
  4752.0 418.8 %reduce-scatter.7.cloned.1.call-start = ((), (), s32[]{:S(2)}) async-start(), calls=%async_computation.7 | async-start | bytes 12582912 | tf_op jit(solution)/shard_map/reduce_scatter | solution.py:264
  4977.6 193.2 %copy-start.18 = (f32[2048]{0:T(1024)S(1)}, f32[2048]{0:T(1024)}, u32[]{:S(2)}) copy-start(f32[2048]{0:T(1024)} %copy-done.16) | copy-start | bytes 24580
  4977.6 193.2 %copy-start.23 = (f32[2048]{0:T(1024)S(1)}, f32[2048]{0:T(1024)}, u32[]{:S(2)}) copy-start(f32[2048]{0:T(1024)} %copy-done.21) | copy-start | bytes 24580
  4977.6 193.2 %copy-start.27 = (f32[2048]{0:T(1024)S(1)}, f32[2048]{0:T(1024)}, u32[]{:S(2)}) copy-start(f32[2048]{0:T(1024)} %copy-done.26) | copy-start | bytes 24580
  4977.6 193.2 %copy-start.29 = (f32[2048]{0:T(1024)S(1)}, f32[2048]{0:T(1024)}, u32[]{:S(2)}) copy-start(f32[2048]{0:T(1024)} %copy-done.28) | copy-start | bytes 24580
  4977.6 193.2 %copy-start.32 = (f32[1024]{0:T(1024)S(1)}, f32[1024]{0:T(1024)}, u32[]{:S(2)}) copy-start(f32[1024]{0:T(1024)} %param.35) | copy-start | bytes 12292
  4977.6 193.2 %copy-start.40 = (f32[1024]{0:T(1024)S(1)}, f32[1024]{0:T(1024)}, u32[]{:S(2)}) copy-start(f32[1024]{0:T(1024)} %param.40) | copy-start | bytes 12292
  5074.7 113.1 %copy-start.35 = (f32[1024]{0:T(1024)S(1)}, f32[1024]{0:T(1024)}, u32[]{:S(2)}) copy-start(f32[1024]{0:T(1024)} %get-tuple-element.546) | copy-start | bytes 12292
  5074.7 113.1 %copy-start.36 = (f32[1024]{0:T(1024)S(1)}, f32[1024]{0:T(1024)}, u32[]{:S(2)}) copy-start(f32[1024]{0:T(1024)} %get-tuple-element.552) | copy-start | bytes 12292
  (241 other events, 764.9 us)
Sparse Core Ops, SparseCore 0:
  17.1 106.6 all-gather.4
  1157.5 99.3 reduce-scatter.4
  1268.8 103.9 all-gather.6
  1374.2 103.9 all-gather.8
  1547.5 99.2 reduce-scatter.8
  1663.8 103.9 all-gather.10
  4733.6 232.6 all-reduce.3
  4969.1 99.3 reduce-scatter.10
  5071.4 99.3 reduce-scatter.6
where the time goes:
time: 5280 us; the launch traced here: 5230 us
  local copies, waits for them, and re-layouts  2110 us (40%)
  matrix products  1870 us (35%)
  waiting for transfers between devices  870 us (16%)
  other arithmetic  290 us (5%)
  blocking collectives  74.8 us (1%)
    reshape x128, local copies, waits for them, and re-layouts, pick_blocks(): picked = picked.reshape(8, per_query, 2, block_rows, head_width)  543 us
    reshape x128, local copies, waits for them, and re-layouts, group_back(): jnp.stack([key_part.reshape(8 * per_query, block_rows * head_width), valu...  373 us
    dot_general x128, matrix products, pick_blocks(): jnp.dot(selector, both_flat, preferred_element_type=jnp.float32)  344 us
    dot_general x64, matrix products, group_back(): lax.dot_general(selector.astype(jnp.float32), parts, ROWWISE, precision=H...  303 us
    mul x64, local copies, waits for them, and re-layouts, group_back(): jnp.einsum('nqk,nqd->nkd', score_grad, query_grp, preferred_element_type=...  207 us
    dot_general x64, matrix products, group_back(): jnp.einsum('nqk,nqd->nkd', probs.astype(jnp.bfloat16), grad_grp, preferre...  200 us
    psum x1, waiting for transfers between devices, per_device(): lax.psum(qkv_grad.astype(jnp.bfloat16), 'dp').astype(jnp.float32)  154 us
    dot_general x64, matrix products, group_back(): jnp.einsum('nqk,nkd->nqd', score_grad, key_grp, preferred_element_type=jn...  154 us
  transfers between devices with their start and end apart: 9, of which 9 were waited for; matrix products, arithmetic and copies ran while one was open for 3% of the time, Pallas kernels for 0%

commit v1 on v0

v1 whole, which is shorter than its diff:
```python
from functools import partial

import jax
import jax.numpy as jnp
from jax import lax
from jax.experimental import pallas as pl
from jax.experimental.pallas import tpu as pltpu
from jax.sharding import PartitionSpec as P

BLOCK = 64


EPSILON = 1e-05
PLAIN = (((1,), (1,)), ((), ()))
ROWWISE = (((0,), (0,)), ((), ()))
HIGH = lax.Precision.HIGHEST


def norm_rows(values, scale_vec, offset):
    centered = values - jnp.mean(values, axis=-1, keepdims=True)
    inv_std = lax.rsqrt(jnp.mean(centered * centered, axis=-1, keepdims=True) + EPSILON)
    normed = centered * inv_std
    return (normed * scale_vec + offset, normed, inv_std)


def norm_back(normed, inv_std, scale_vec, gradient):
    scaled = gradient * scale_vec
    inner_term = (
        scaled
        - jnp.mean(scaled, axis=-1, keepdims=True)
        - normed * jnp.mean(scaled * normed, axis=-1, keepdims=True)
    )
    return (inv_std * inner_term, jnp.sum(gradient * normed, 0), jnp.sum(gradient, 0))


def gelu_tanh(values):
    return jax.nn.gelu(values, approximate=True)


NT = (((1,), (1,)), ((), ()))
F32 = jnp.float32
BF16 = jnp.bfloat16
UNROLL_F = 2
UNROLL_B = 2


def mm(a, b):
    return jnp.dot(a, b, preferred_element_type=F32)


def mm_nt(a, b):
    return lax.dot_general(a, b, NT, preferred_element_type=F32)


def lane_left(rows, lanes=128):
    return lax.broadcasted_iota(jnp.int32, (rows, lanes), 1) % 128 < BLOCK


def fill_transposed(src_ref, out_ref, num_blocks):
    def one(j, c):
        t = src_ref[pl.ds(j * 128, 128), :].astype(F32).T
        out_ref[2 * j] = t.astype(BF16)
        out_ref[2 * j + 1] = pltpu.roll(t, BLOCK, 1).astype(BF16)
        return c
    lax.fori_loop(0, num_blocks // 2, one, 0, unroll=2)


def block_diag(x):
    left = lane_left(BLOCK)
    zero = jnp.zeros_like(x)
    return jnp.concatenate([jnp.where(left, x, zero), jnp.where(left, zero, x)], 0)


def rows_of(ref, b):
    return ref[pl.ds(pl.multiple_of(b * BLOCK, BLOCK), BLOCK), :]


def gather_rows(ref, i, pairs, num_blocks):
    left = lane_left(BLOCK)
    parts = [
        ref[0:BLOCK, :],
        ref[(num_blocks - 1) * BLOCK:, :],
        ref[pl.ds(pl.multiple_of((i - 1) * BLOCK, BLOCK), 3 * BLOCK), :],
    ]
    for a, b in pairs:
        parts.append(jnp.where(left, rows_of(ref, a), rows_of(ref, b)))
    return jnp.concatenate(parts, 0)


def gather_cols(tr, i, pairs, num_blocks):
    left = lane_left(128)

    def side(a, b):
        if a is b:
            return tr[a]
        return jnp.concatenate([tr[a, 0:BLOCK, :], tr[b, BLOCK:, :]], 0)

    def tile(first, second):
        return jnp.where(left, side(*first), side(second[0] ^ 1, second[1] ^ 1) if second[0] is not second[1] else tr[second[0] ^ 1])

    end = num_blocks - 1
    lo, hi = i - 1, i + 1
    r = pairs
    return jnp.concatenate([
        tile((0, 0), (end, end)),
        tile((lo, lo), (i, i)),
        tile((hi, hi), r[0]),
        tile(r[1], r[2]),
    ], 1)


def fwd_kernel(rand_ref, q_ref, k_ref, v_ref, o_ref, lse_ref, vt, *, scale):
    p = pl.program_id(0)
    num_blocks = q_ref.shape[0] // BLOCK
    fill_transposed(v_ref, vt, num_blocks)
    left = lane_left(BLOCK)
    inner = num_blocks - 2

    def qd(i):
        return block_diag(rows_of(q_ref, i) * jnp.asarray(scale, BF16))

    def finish(i, ot, m, l):
        o = (ot * (1.0 / l)).T
        o_ref[pl.ds(pl.multiple_of(i * BLOCK, BLOCK), BLOCK), :] = jnp.where(
            left, o[:BLOCK], o[BLOCK:]).astype(BF16)
        lse_ref[0, pl.ds(i, 1), :] = m + jnp.log(l)

    def regular(i):
        pairs = [(rand_ref[2 * p, (i - 1) * 3 + t], rand_ref[2 * p + 1, (i - 1) * 3 + t]) for t in range(3)]
        s = mm_nt(gather_rows(k_ref, i, pairs, num_blocks), qd(i))
        m = jnp.max(s, 0, keepdims=True)
        e = jnp.exp(s - m)
        l = jnp.sum(e, 0, keepdims=True)
        ot = mm(gather_cols(vt, i, pairs, num_blocks), e.astype(BF16))
        finish(i, ot, m, l)

    def step(n, c):
        for u in range(UNROLL_F):
            regular(1 + n * UNROLL_F + u)
        return c

    lax.fori_loop(0, inner // UNROLL_F, step, 0)
    for i in range(1 + inner // UNROLL_F * UNROLL_F, num_blocks - 1):
        regular(i)

    ends = (0, num_blocks - 1)
    qs = [qd(i) for i in ends]

    def chunk(c, carry):
        kc = k_ref[pl.ds(pl.multiple_of(c * 512, 512), 512), :]
        vc = jnp.concatenate([vt[c * 8 + 2 * t] for t in range(4)], 1)
        out = []
        for (m, l, acc), qb in zip(carry, qs):
            s = mm_nt(kc, qb)
            m2 = jnp.maximum(m, jnp.max(s, 0, keepdims=True))
            a = jnp.exp(m - m2)
            e = jnp.exp(s - m2)
            out.append((m2, l * a + jnp.sum(e, 0, keepdims=True), acc * a + mm(vc, e.astype(BF16))))
        return tuple(out)

    init = (jnp.full((1, 128), -jnp.inf, F32), jnp.zeros((1, 128), F32), jnp.zeros((128, 128), F32))
    res = lax.fori_loop(0, num_blocks * BLOCK // 512, chunk, (init, init))
    for i, (m, l, acc) in zip(ends, res):
        finish(i, acc, m, l)


def attend_fwd(rand2, qkv):
    rows, pairs = qkv.shape[1], qkv.shape[2] // 128
    num_blocks = rows // BLOCK

    def spec(which):
        return pl.BlockSpec((None, rows, 128), lambda p, r: (which, 0, p))

    return pl.pallas_call(
        partial(fwd_kernel, scale=BLOCK**-0.5),
        out_shape=(
            jax.ShapeDtypeStruct((rows, pairs * 128), BF16),
            jax.ShapeDtypeStruct((pairs, num_blocks, 128), F32),
        ),
        grid_spec=pltpu.PrefetchScalarGridSpec(
            num_scalar_prefetch=1,
            grid=(pairs,),
            in_specs=[spec(0), spec(1), spec(2)],
            out_specs=(
                pl.BlockSpec((rows, 128), lambda p, r: (0, p)),
                pl.BlockSpec((1, num_blocks, 128), lambda p, r: (p, 0, 0)),
            ),
            scratch_shapes=[pltpu.VMEM((num_blocks, 128, 128), BF16)],
        ),
        compiler_params=pltpu.CompilerParams(vmem_limit_bytes=60 << 20),
        cost_estimate=pl.CostEstimate(
            flops=pairs * num_blocks * 2 * 2 * 512 * 128 * 128,
            bytes_accessed=pairs * rows * 128 * 2 * 4,
            transcendentals=pairs * num_blocks * 512 * 128,
        ),
        name="attend_fwd",
    )(rand2, qkv, qkv, qkv)


def bwd_kernel(rand_ref, q_ref, k_ref, v_ref, do_ref, o_ref, lse_ref, out_ref, kt, acc, *, scale):
    p = pl.program_id(0)
    num_blocks = q_ref.shape[0] // BLOCK
    fill_transposed(k_ref, kt, num_blocks)
    left = lane_left(BLOCK)
    inner = num_blocks - 2
    sc = jnp.asarray(scale, BF16)
    acc[...] = jnp.zeros_like(acc)
    zero = jnp.zeros((BLOCK, 128), BF16)

    def operands(i):
        qi = rows_of(q_ref, i) * sc
        gi = rows_of(do_ref, i)
        ql, qr = jnp.where(left, qi, zero), jnp.where(left, zero, qi)
        gl, gr = jnp.where(left, gi, zero), jnp.where(left, zero, gi)
        qx = jnp.concatenate([qi[:, BLOCK:], qi[:, :BLOCK]], 1)
        gx = jnp.concatenate([gi[:, BLOCK:], gi[:, :BLOCK]], 1)
        score_rhs = jnp.concatenate([
            jnp.concatenate([ql, zero], 1), jnp.concatenate([qr, zero], 1),
            jnp.concatenate([zero, gl], 1), jnp.concatenate([zero, gr], 1)], 0)
        grad_rhs = jnp.concatenate([
            jnp.concatenate([gl, zero], 1), jnp.concatenate([zero, jnp.where(left, gx, zero)], 1),
            jnp.concatenate([jnp.where(left, zero, qx), zero], 1), jnp.concatenate([zero, qr], 1)], 0)
        return score_rhs, grad_rhs

    def grads(kv, score_rhs, grad_rhs, lse, delta):
        sd = mm_nt(kv, score_rhs)
        pr = jnp.exp(sd[:, :128] - lse)
        dp = sd[:, 128:]
        if delta is None:
            delta = jnp.sum(pr * dp, 0, keepdims=True)
        ds = (pr * (dp - delta)).astype(BF16)
        c = mm(jnp.concatenate([pr.astype(BF16), ds], 1), grad_rhs)
        return ds, c

    def put_dq(i, dqt):
        dq = dqt.T
        out_ref[0, pl.ds(pl.multiple_of(i * BLOCK, BLOCK), BLOCK), :] = (jnp.where(
            left, dq[:BLOCK], dq[BLOCK:]) * scale).astype(BF16)

    def regular(i):
        pairs = [(rand_ref[2 * p, (i - 1) * 3 + t], rand_ref[2 * p + 1, (i - 1) * 3 + t]) for t in range(3)]
        kv = jnp.concatenate([gather_rows(k_ref, i, pairs, num_blocks), gather_rows(v_ref, i, pairs, num_blocks)], 1)
        ds, c = grads(kv, *operands(i), lse_ref[0, pl.ds(i, 1), :], None)
        put_dq(i, mm(gather_cols(kt, i, pairs, num_blocks), ds))
        acc[0:BLOCK, :] += c[0:BLOCK]
        acc[(num_blocks - 1) * BLOCK:, :] += c[BLOCK:2 * BLOCK]
        acc[pl.ds(pl.multiple_of((i - 1) * BLOCK, BLOCK), 3 * BLOCK), :] += c[2 * BLOCK:5 * BLOCK]
        for t, (a, b) in enumerate(pairs):
            acc[pl.ds(pl.multiple_of(a * BLOCK, BLOCK), BLOCK), 0:128] += c[(5 + t) * BLOCK:(6 + t) * BLOCK, :128]
            acc[pl.ds(pl.multiple_of(b * BLOCK, BLOCK), BLOCK), 128:256] += c[(5 + t) * BLOCK:(6 + t) * BLOCK, 128:]

    def step(n, c):
        for u in range(UNROLL_B):
            regular(1 + n * UNROLL_B + u)
        return c

    lax.fori_loop(0, inner // UNROLL_B, step, 0)
    for i in range(1 + inner // UNROLL_B * UNROLL_B, num_blocks - 1):
        regular(i)

    for i in (0, num_blocks - 1):
        score_rhs, grad_rhs = operands(i)
        t = (rows_of(do_ref, i).astype(F32) * rows_of(o_ref, i).astype(F32)).T
        delta = jnp.concatenate([jnp.sum(t[:BLOCK], 0, keepdims=True), jnp.sum(t[BLOCK:], 0, keepdims=True)], 1)
        lse = lse_ref[0, i:i + 1, :]

        def chunk(c, dqt, score_rhs=score_rhs, grad_rhs=grad_rhs, lse=lse, delta=delta):
            at = pl.ds(pl.multiple_of(c * 512, 512), 512)
            kv = jnp.concatenate([k_ref[at, :], v_ref[at, :]], 1)
            ds, out = grads(kv, score_rhs, grad_rhs, lse, delta)
            acc[at, :] += out
            return dqt + mm(jnp.concatenate([kt[c * 8 + 2 * t] for t in range(4)], 1), ds)

        put_dq(i, lax.fori_loop(0, num_blocks * BLOCK // 512, chunk, jnp.zeros((128, 128), F32)))

    big = lane_left(512)

    def out(c, _):
        at = pl.ds(pl.multiple_of(c * 512, 512), 512)
        a0, a1 = acc[at, 0:128], acc[at, 128:256]
        out_ref[2, at, :] = jnp.where(big, a0, pltpu.roll(a1, BLOCK, 1)).astype(BF16)
        out_ref[1, at, :] = jnp.where(big, pltpu.roll(a0, BLOCK, 1), a1).astype(BF16)
        return _

    lax.fori_loop(0, num_blocks * BLOCK // 512, out, 0)


def attend_bwd(rand2, qkv, do, o, lse):
    rows, pairs = qkv.shape[1], qkv.shape[2] // 128
    num_blocks = rows // BLOCK

    def spec(which):
        return pl.BlockSpec((None, rows, 128), lambda p, r: (which, 0, p))

    flat = pl.BlockSpec((rows, 128), lambda p, r: (0, p))
    return pl.pallas_call(
        partial(bwd_kernel, scale=BLOCK**-0.5),
        out_shape=jax.ShapeDtypeStruct((3, rows, pairs * 128), BF16),
        grid_spec=pltpu.PrefetchScalarGridSpec(
            num_scalar_prefetch=1,
            grid=(pairs,),
            in_specs=[
                spec(0),
                spec(1),
                spec(2),
                flat,
                flat,
                pl.BlockSpec((1, num_blocks, 128), lambda p, r: (p, 0, 0)),
            ],
            out_specs=pl.BlockSpec((3, rows, 128), lambda p, r: (0, 0, p)),
            scratch_shapes=[
                pltpu.VMEM((num_blocks, 128, 128), BF16),
                pltpu.VMEM((rows, 256), F32),
            ],
        ),
        compiler_params=pltpu.CompilerParams(vmem_limit_bytes=60 << 20),
        cost_estimate=pl.CostEstimate(
            flops=pairs * num_blocks * 2 * 5 * 512 * 128 * 128,
            bytes_accessed=pairs * rows * 128 * 2 * 8,
            transcendentals=pairs * num_blocks * 512 * 128,
        ),
        name="attend_bwd",
    )(rand2, qkv, qkv, qkv, do, o, lse)


def per_device(
    inputs,
    rand_blocks,
    ln1_gain,
    ln1_bias,
    w_qkv,
    w_out,
    ln2_gain,
    ln2_bias,
    w_up,
    b_up,
    w_down,
    b_down,
    cotangent,
):
    seqs_here = rand_blocks.shape[0]
    heads_here = rand_blocks.shape[1]
    residual_in = inputs.astype(jnp.float32)
    normed_one, normed_a, inv_a = norm_rows(residual_in, ln1_gain, ln1_bias)
    first_rows = lax.all_gather(normed_one.astype(jnp.bfloat16), "mp", axis=0, tiled=True)
    group_rows = first_rows.shape[0]
    seq_len = group_rows // seqs_here
    projected = jnp.einsum(
        "td,cde->cte", first_rows, w_qkv, preferred_element_type=jnp.float32
    ).astype(jnp.bfloat16)
    tables = rand_blocks.reshape(seqs_here, heads_here, -1)
    qkv_seqs = [projected[:, n * seq_len : (n + 1) * seq_len] for n in range(seqs_here)]
    fwd_seqs = [attend_fwd(tables[n], qkv_seqs[n]) for n in range(seqs_here)]
    attn_mix = jnp.concatenate([o for o, _ in fwd_seqs], 0)
    attn_out = lax.psum_scatter(
        jnp.dot(attn_mix, w_out, preferred_element_type=jnp.float32).astype(jnp.bfloat16),
        "mp",
        scatter_dimension=0,
        tiled=True,
    ).astype(jnp.float32)
    mid_resid = residual_in + attn_out
    normed_two, normed_b, inv_b = norm_rows(mid_resid, ln2_gain, ln2_bias)
    second_rows, grad_rows = (
        lax.all_gather(normed_two.astype(jnp.bfloat16), "mp", axis=0, tiled=True),
        lax.all_gather(cotangent, "mp", axis=0, tiled=True),
    )
    hidden_pre = jnp.dot(second_rows, w_up, preferred_element_type=jnp.float32) + b_up
    hidden_act = gelu_tanh(hidden_pre).astype(jnp.bfloat16)
    branch_out = lax.psum_scatter(
        jnp.dot(hidden_act, w_down, preferred_element_type=jnp.float32).astype(jnp.bfloat16),
        "mp",
        scatter_dimension=0,
        tiled=True,
    ).astype(jnp.float32)
    result = mid_resid + (branch_out + b_down)
    grad_own = cotangent.astype(jnp.float32)
    bias_down_grad = jnp.sum(grad_own, 0)
    down_grad = lax.dot_general(hidden_act, grad_rows, ROWWISE, preferred_element_type=jnp.float32)
    act_grad = lax.dot_general(grad_rows, w_down, PLAIN, preferred_element_type=jnp.float32)
    gelu_pull = jax.vjp(gelu_tanh, hidden_pre)[1]
    pre_grad = gelu_pull(act_grad)[0].astype(jnp.bfloat16)
    bias_up_grad = jnp.sum(pre_grad.astype(jnp.float32), 0)
    up_grad = lax.dot_general(second_rows, pre_grad, ROWWISE, preferred_element_type=jnp.float32)
    second_grad = lax.psum_scatter(
        lax.dot_general(pre_grad, w_up, PLAIN, preferred_element_type=jnp.float32).astype(
            jnp.bfloat16
        ),
        "mp",
        scatter_dimension=0,
        tiled=True,
    ).astype(jnp.float32)
    mid_part, gain_two_grad, bias_two_grad = norm_back(normed_b, inv_b, ln2_gain, second_grad)
    mid_grad = grad_own + mid_part
    attn_grad_rows = lax.all_gather(mid_grad.astype(jnp.bfloat16), "mp", axis=0, tiled=True)
    out_grad = lax.dot_general(
        attn_mix, attn_grad_rows, ROWWISE, preferred_element_type=jnp.float32
    )
    mix_grad = lax.dot_general(
        attn_grad_rows, w_out, PLAIN, preferred_element_type=jnp.float32
    ).astype(jnp.bfloat16)
    stacked = jnp.concatenate(
        [
            attend_bwd(
                tables[n],
                qkv_seqs[n],
                mix_grad[n * seq_len : (n + 1) * seq_len],
                fwd_seqs[n][0],
                fwd_seqs[n][1],
            )
            for n in range(seqs_here)
        ],
        1,
    )
    qkv_grad = jnp.einsum("td,cte->cde", first_rows, stacked, preferred_element_type=jnp.float32)
    first_grad = lax.psum_scatter(
        jnp.einsum("cte,cde->td", stacked, w_qkv, preferred_element_type=jnp.float32).astype(
            jnp.bfloat16
        ),
        "mp",
        scatter_dimension=0,
        tiled=True,
    ).astype(jnp.float32)
    input_part, gain_one_grad, bias_one_grad = norm_back(normed_a, inv_a, ln1_gain, first_grad)
    input_grad = mid_grad + input_part
    small_sums = lax.psum(
        (gain_one_grad, bias_one_grad, gain_two_grad, bias_two_grad, bias_down_grad), ("dp", "mp")
    )
    qkv_grad, out_grad, up_grad, bias_up_grad, down_grad = (
        lax.psum(qkv_grad.astype(jnp.bfloat16), "dp").astype(jnp.float32),
        lax.psum(out_grad.astype(jnp.bfloat16), "dp").astype(jnp.float32),
        lax.psum(up_grad.astype(jnp.bfloat16), "dp").astype(jnp.float32),
        lax.psum(bias_up_grad.astype(jnp.bfloat16), "dp").astype(jnp.float32),
        lax.psum(down_grad.astype(jnp.bfloat16), "dp").astype(jnp.float32),
    )
    return (
        result,
        input_grad,
        small_sums[0],
        small_sums[1],
        qkv_grad,
        out_grad,
        small_sums[2],
        small_sums[3],
        up_grad,
        bias_up_grad,
        down_grad,
        small_sums[4],
    )


def solution(mesh):
    return jax.shard_map(
        per_device,
        mesh=mesh,
        in_specs=(
            P(("dp", "mp"), None),
            P("dp", "mp", None, None),
            P(),
            P(),
            P(None, None, "mp"),
            P("mp", None),
            P(),
            P(),
            P(None, "mp"),
            P("mp"),
            P("mp", None),
            P(),
            P(("dp", "mp"), None),
        ),
        out_specs=(
            P(("dp", "mp"), None),
            P(("dp", "mp"), None),
            P(),
            P(),
            P(None, None, "mp"),
            P("mp", None),
            P(),
            P(),
            P(None, "mp"),
            P("mp"),
            P("mp", None),
            P(),
        ),
        check_vma=False,
    )
```

time: 5280 us -> 1650 us (0.31)
  local copies, waits for them, and re-layouts: 2110 us -> 10.2 us
  matrix products: 1870 us -> 259 us
  Pallas kernels: 0 us -> 346 us
  other arithmetic: 290 us -> 73.4 us
    dot_general x696 -> x0, matrix products: 1610 us -> none  [the longest x128 344 us: pick_blocks(): jnp.dot(selector, both_flat, preferred_element_type=jnp.float32)]
    reshape x410 -> x0, local copies, waits for them, and re-layouts: 1240 us -> none  [the longest x128 543 us: pick_blocks(): picked = picked.reshape(8, per_query, 2, block_rows, head_width)]
    pallas_call x0 -> x2, Pallas kernels: none -> 346 us  [the longest x1 206 us: attend_bwd(): pl.pallas_call(partial(bwd_kernel, scale=BLOCK ** (-0.5)), out_shape=jax....]
    slice x160 -> x0, local copies, waits for them, and re-layouts: 273 us -> none  [the longest x64 110 us: pick_blocks(): key_grp = picked[:, :, 0].reshape(8, per_query * block_rows, head_width)]
    mul x64 -> x0, local copies, waits for them, and re-layouts: 207 us -> none  [group_back(): jnp.einsum('nqk,nqd->nkd', score_grad, query_grp, preferred_element_type=...]
    while x88 -> x0, other arithmetic: 129 us -> none
    while x433 -> x0, local copies, waits for them, and re-layouts: 120 us -> none
    dynamic_slice x160 -> x0, local copies, waits for them, and re-layouts: 84.6 us -> none  [the longest x32 84.4 us: per_device(): lax.map(attend_item, (heads_qkv[0], heads_qkv[1], heads_qkv[2], tables))]
  transfers between devices with their start and end apart: 9 -> 9, of which waited for: 9 -> 9; matrix products, arithmetic and copies ran while one was open for 3% -> 9% of each run, Pallas kernels for 0% -> 0%
where the time goes in v1:
time: 1650 us
  waiting for transfers between devices  869 us (53%)
  Pallas kernels  346 us (21%)
  matrix products  259 us (16%)
  blocking collectives  74.6 us (5%)
  other arithmetic  73.4 us (4%)
    pallas_call x1, Pallas kernels, attend_bwd(): pl.pallas_call(partial(bwd_kernel, scale=BLOCK ** (-0.5)), out_shape=jax....  206 us
    psum x1, waiting for transfers between devices, per_device(): lax.psum(qkv_grad.astype(jnp.bfloat16), 'dp').astype(jnp.float32)  155 us
    pallas_call x1, Pallas kernels, attend_fwd(): pl.pallas_call(partial(fwd_kernel, scale=BLOCK ** (-0.5)), out_shape=(jax...  140 us
    all_gather x1, waiting for transfers between devices, per_device(): lax.all_gather(normed_one.astype(jnp.bfloat16), 'mp', axis=0, tiled=True)  106 us
    all_gather x1, waiting for transfers between devices, per_device(): lax.all_gather(normed_two.astype(jnp.bfloat16), 'mp', axis=0, tiled=True)  104 us
    reduce_scatter x1, waiting for transfers between devices, per_device(): lax.psum_scatter(lax.dot_general(pre_grad, w_up, PLAIN, preferred_element...  99.4 us
    reduce_scatter x1, waiting for transfers between devices, per_device(): lax.psum_scatter(jnp.dot(attn_mix, w_out, preferred_element_type=jnp.floa...  98.9 us
    reduce_scatter x1, waiting for transfers between devices, per_device(): lax.psum_scatter(jnp.dot(hidden_act, w_down, preferred_element_type=jnp.f...  96.1 us
  transfers between devices with their start and end apart: 9, of which 9 were waited for; matrix products, arithmetic and copies ran while one was open for 9% of the time, Pallas kernels for 0%

profile of v1, /device:TPU:0, one launch (start us, length us, event | category | flops | bytes accessed | tf_op | source)
XLA Modules:
  0.0 1647.9 jit_solution(15165237510670386677)
XLA Ops:
  18.2 105.7 %all-gather.5.cloned.1.call-done = bf16[4096,1024]{1,0:T(8,128)(2,1)} async-done(((bf16[2048,1024]{1,0:T(8,128)(2,1)}), bf16[4096,1024]{1,0:T(8,128)(2,1)}) %all-gather.5.cloned.1.call-update) | async-done | bytes 8388624 | tf_op jit(solution)/shard_map/all_gather | solution.py:345
  123.9 19.0 %convert_bitcast_fusion.q_ref.k_ref.v_ref = bf16[3,4096,512]{2,1,0:T(8,128)(2,1)} fusion(bf16[3,1024,512]{2,1,0:T(8,128)(2,1)S(1)} %copy-done, bf16[4096,1024]{1,0:T(8,128)(2,1)} %all-gather.5.cloned.1.call-done), kind=kOutput, calls=%fused_computation.17 | convolution fusion | flops 12891193344 | bytes 24117248 | tf_op jit(solution)/shard_map/td,cde->cte/dot_general | solution.py:348
  142.9 140.4 %attend_fwd.1 = (bf16[4096,512]{1,0:T(8,128)(2,1)}, f32[4,64,128]{2,1,0:T(8,128)}) custom-call(s32[8,186]{1,0:T(8,128)} %copy.29.rand_ref, bf16[3,4096,512]{2,1,0:T(8,128)(2,1)} %convert_bitcast_fusion.q_ref.k_ref.v_ref, bf16[3,4096,512]{2,1,0:T(8,128)(2,1)} %convert_bitcast_fusion.q_ref.k_ref.v_ref, bf16[3,4096,512]{2,1,0:T(8,128)(2,1)} %convert_bitcast_fusion.q_ref.k_ref.v_ref), custom_call_target="tpu_custom_call" | custom-call | flops 8589934592 | bytes 16777216 | tf_op jit(solution)/shard_map/attend_fwd/pallas_call | solution.py:174
  283.2 10.4 convolution_convert_fusion.2
  294.3 98.9 %reduce-scatter.5.cloned.1.call-done = bf16[2048,1024]{1,0:T(8,128)(2,1)} async-done(((bf16[4096,1024]{1,0:T(8,128)(2,1)}), bf16[2048,1024]{1,0:T(8,128)(2,1)}) %reduce-scatter.5.cloned.1.call-update) | async-done | bytes 4194320 | tf_op jit(solution)/shard_map/reduce_scatter | solution.py:355
  405.6 103.5 %all-gather.7.cloned.1.call-done = bf16[4096,1024]{1,0:T(8,128)(2,1)} async-done(((bf16[2048,1024]{1,0:T(8,128)(2,1)}), bf16[4096,1024]{1,0:T(8,128)(2,1)}) %all-gather.7.cloned.1.call-update) | async-done | bytes 8388624 | tf_op jit(solution)/shard_map/all_gather | solution.py:364
  509.1 33.9 %multiply_convert_fusion = (bf16[4096,2048]{1,0:T(8,128)(2,1)}, f32[4096,2048]{1,0:T(8,128)}) fusion(f32[2048]{0:T(1024)S(1)} %copy-done.34, bf16[4096,1024]{1,0:T(8,128)(2,1)} %all-gather.7.cloned.1.call-done, bf16[1024,2048]{1,0:T(8,128)(2,1)} %param.21), kind=kOutput, calls=%fused_computation.9 | convolution fusion | flops 17263755264 | bytes 62922752 | tf_op jit(solution)/shard_map/dot_general | solution.py:367
  543.0 71.5 %all-gather.9.cloned.1.call-done = bf16[4096,1024]{1,0:T(8,128)(2,1)} async-done(((bf16[2048,1024]{1,0:T(8,128)(2,1)}), bf16[4096,1024]{1,0:T(8,128)(2,1)}) %all-gather.9.cloned.1.call-update) | async-done | bytes 8388624 | tf_op jit(solution)/shard_map/all_gather | solution.py:365
  614.5 45.2 %fusion.36 = (bf16[2048]{0:T(1024)(128)(2,1)}, bf16[4096,2048]{1,0:T(8,128)(2,1)}) fusion(f32[4096,2048]{1,0:T(8,128)} %get-tuple-element.61, f32[2048]{0:T(1024)S(1)} %copy-done.34, bf16[4096,1024]{1,0:T(8,128)(2,1)} %all-gather.9.cloned.1.call-done, bf16[2048,1024]{1,0:T(8,128)(2,1)} %param.23), kind=kOutput, calls=%fused_computation.70 | convolution fusion | flops 17364416512 | bytes 62926848 | tf_op jit(solution)/shard_map/dot_general | solution.py:379
  659.8 23.7 %convolution_convert_fusion = bf16[4096,1024]{1,0:T(8,128)(2,1)} fusion(bf16[4096,2048]{1,0:T(8,128)(2,1)} %get-tuple-element.63, bf16[1024,2048]{1,0:T(8,128)(2,1)} %param.21), kind=kOutput, calls=%fused_computation.52 | convolution fusion | flops 17184063488 | bytes 29360128 | tf_op jit(solution)/shard_map/dot_general | solution.py:385
  683.6 99.4 %reduce-scatter.9.cloned.1.call-done = bf16[2048,1024]{1,0:T(8,128)(2,1)} async-done(((bf16[4096,1024]{1,0:T(8,128)(2,1)}), bf16[2048,1024]{1,0:T(8,128)(2,1)}) %reduce-scatter.9.cloned.1.call-update) | async-done | bytes 4194320 | tf_op jit(solution)/shard_map/reduce_scatter | solution.py:384
  800.0 24.2 %convolution_convert_fusion.5 = bf16[1024,2048]{1,0:T(8,128)(2,1)} fusion(bf16[4096,1024]{1,0:T(8,128)(2,1)} %all-gather.7.cloned.1.call-done, bf16[4096,2048]{1,0:T(8,128)(2,1)} %get-tuple-element.63), kind=kOutput, calls=%fused_computation.58 | convolution fusion | flops 17181966336 | bytes 29360128 | tf_op jit(solution)/shard_map/dot_general | solution.py:383
  824.2 23.7 %convolution_convert_fusion.4 = bf16[2048,1024]{1,0:T(8,128)(2,1)} fusion(bf16[4096,2048]{1,0:T(8,128)(2,1)} %get-tuple-element.60, bf16[4096,1024]{1,0:T(8,128)(2,1)} %all-gather.9.cloned.1.call-done), kind=kOutput, calls=%fused_computation.57 | convolution fusion | flops 17181966336 | bytes 29360128 | tf_op jit(solution)/shard_map/dot_general | solution.py:378
  847.9 56.2 %all-gather.11.cloned.1.call-done = bf16[4096,1024]{1,0:T(8,128)(2,1)} async-done(((bf16[2048,1024]{1,0:T(8,128)(2,1)}), bf16[4096,1024]{1,0:T(8,128)(2,1)}) %all-gather.11.cloned.1.call-update) | async-done | bytes 8388624 | tf_op jit(solution)/shard_map/all_gather | solution.py:394
  914.3 205.8 %attend_bwd.1 = bf16[3,4096,512]{2,1,0:T(8,128)(2,1)} custom-call(s32[8,186]{1,0:T(8,128)} %copy.29.rand_ref, bf16[3,4096,512]{2,1,0:T(8,128)(2,1)} %convert_bitcast_fusion.q_ref.k_ref.v_ref, bf16[3,4096,512]{2,1,0:T(8,128)(2,1)} %convert_bitcast_fusion.q_ref.k_ref.v_ref, bf16[3,4096,512]{2,1,0:T(8,128)(2,1)} %convert_bitcast_fusion.q_ref.k_ref.v_ref, ...), custom_call_target="tpu_custom_call" | custom-call | flops 21474836480 | bytes 33554432 | tf_op jit(solution)/shard_map/attend_bwd/pallas_call | solution.py:296
  1130.4 16.5 %convert_bitcast_fusion.1 = bf16[3,1024,512]{1,2,0:T(8,128)(2,1)} fusion(bf16[3,4096,512]{2,1,0:T(8,128)(2,1)S(1)} %copy-done.35, bf16[4096,1024]{1,0:T(8,128)(2,1)} %all-gather.5.cloned.1.call-done), kind=kOutput, calls=%fused_computation.59 | convolution fusion | flops 12886474752 | bytes 24117248 | tf_op jit(solution)/shard_map/td,cte->cde/dot_general | solution.py:414
  1147.0 18.5 %bitcast_convert_fusion = bf16[4096,1024]{1,0:T(8,128)(2,1)} fusion(bf16[3,4096,512]{2,1,0:T(8,128)(2,1)} %attend_bwd.1, bf16[3,1024,512]{2,1,0:T(8,128)(2,1)S(1)} %copy-done), kind=kOutput, calls=%fused_computation.10 | convolution fusion | flops 12889096192 | bytes 24117248 | tf_op jit(solution)/shard_map/cte,cde->td/dot_general | solution.py:416
  1165.5 23.6 %convolution_convert_fusion.1 = bf16[4096,1024]{1,0:T(8,128)(2,1)} fusion(bf16[4096,2048]{1,0:T(8,128)(2,1)} %get-tuple-element.60, bf16[2048,1024]{1,0:T(8,128)(2,1)} %param.23), kind=kOutput, calls=%fused_computation.53 | convolution fusion | flops 17184063488 | bytes 29360128 | tf_op jit(solution)/shard_map/dot_general | solution.py:370
  1189.8 34.8 %psum.77 = bf16[2048]{0:T(1024)(128)(2,1)S(1)} all-reduce(bf16[2048]{0:T(1024)(128)(2,1)S(1)} %copy-done.33), channel_id=1, replica_groups=mesh['dp'=16,'mp'=2] {'dp'}, use_global_device_ids=true, to_apply=%region_24.0 | all-reduce | flops 2048 | bytes 8192 | tf_op jit(solution)/shard_map/psum | solution.py:432
  1225.2 154.5 %all-reduce.4.cloned.1.call-done = (bf16[3,1024,512]{1,2,0:T(8,128)(2,1)}, bf16[512,1024]{1,0:T(8,128)(2,1)}, bf16[1024,2048]{1,0:T(8,128)(2,1)}, bf16[2048,1024]{1,0:T(8,128)(2,1)}) async-done(((bf16[3,1024,512]{1,2,0:T(8,128)(2,1)}, bf16[512,1024]{1,0:T(8,128)(2,1)}, bf16[1024,2048]{1,0:T(8,128)(2,1)}, bf16[2048,1024]{1,0:T(8,128)(2,1)}), (bf16[3,1024,512]{1,2,0:T(8,128)(2,1)}, ...) | async-done | bytes 12582928 | tf_op jit(solution)/shard_map/psum | solution.py:429
  1399.8 82.2 %reduce-scatter.11.cloned.1.call-done = bf16[2048,1024]{1,0:T(8,128)(2,1)} async-done(((bf16[4096,1024]{1,0:T(8,128)(2,1)}), bf16[2048,1024]{1,0:T(8,128)(2,1)}) %reduce-scatter.11.cloned.1.call-update) | async-done | bytes 4194320 | tf_op jit(solution)/shard_map/reduce_scatter | solution.py:415
  1488.1 96.1 %reduce-scatter.7.cloned.1.call-done = bf16[2048,1024]{1,0:T(8,128)(2,1)} async-done(((bf16[4096,1024]{1,0:T(8,128)(2,1)}), bf16[2048,1024]{1,0:T(8,128)(2,1)}) %reduce-scatter.7.cloned.1.call-update) | async-done | bytes 4194320 | tf_op jit(solution)/shard_map/reduce_scatter | solution.py:369
  1584.2 17.0 %fusion.21 = (f32[2048,1024]{1,0:T(8,128)}, f32[2048,1024]{1,0:T(8,128)}, f32[1024]{0:T(1024)S(1)}) fusion(bf16[2048,1024]{1,0:T(8,128)(2,1)} %param.13, bf16[2048,1024]{1,0:T(8,128)(2,1)} %reduce-scatter.11.cloned.1.call-done, f32[2048]{0:T(1024)S(1)} %broadcast_multiply_fusion, f32[2048]{0:T(1024)S(1)} %broadcast_multiply_fusion.1, ...), kind=kLoop, calls=%fused_computation.37 | loop fusion | flops 54524928 | bytes 42024960 | tf_op jit(solution)/shard_map/add | solution.py:424
  1601.2 39.9 %all-reduce = (f32[1024]{0:T(1024)}, f32[1024]{0:T(1024)}, f32[1024]{0:T(1024)}, f32[1024]{0:T(1024)}, f32[1024]{0:T(1024)}) all-reduce(f32[1024]{0:T(1024)S(1)} %get-tuple-element.42, f32[1024]{0:T(1024)S(1)} %get-tuple-element.47, f32[1024]{0:T(1024)S(1)} %copy-done.27, ...), channel_id=1, replica_groups=mesh['dp'=16,'mp'=2] {'dp','mp'}, use_global_device_ids=true, to_apply=%region_13.0 | all-reduce | flops 5120 | bytes 40960 | tf_op jit(solution)/shard_map/psum | solution.py:425
  (116 shorter events, 88.9 us)
Async XLA Ops:
  7.2 116.7 %copy-start = (bf16[3,1024,512]{2,1,0:T(8,128)(2,1)S(1)}, bf16[3,1024,512]{2,1,0:T(8,128)(2,1)}, u32[]{:S(2)}) copy-start(bf16[3,1024,512]{2,1,0:T(8,128)(2,1)} %param.17) | copy-start | bytes 9437188
  7.2 116.6 %all-gather.5.cloned.1.call-start = ((), (), s32[]{:S(2)}) async-start(), calls=%async_computation.4 | async-start | bytes 12582912 | tf_op jit(solution)/shard_map/all_gather | solution.py:345
  17.0 376.2 %reduce-scatter.5.cloned.1.call-start = ((), (), s32[]{:S(2)}) async-start(), calls=%async_computation.5 | async-start | bytes 12582912 | tf_op jit(solution)/shard_map/reduce_scatter | solution.py:355
  293.7 107.8 %copy-start.22 = (f32[1024]{0:T(1024)S(1)}, f32[1024]{0:T(1024)}, u32[]{:S(2)}) copy-start(f32[1024]{0:T(1024)} %param.19) | copy-start | bytes 12292
  293.7 107.8 %copy-start.31 = (f32[1024]{0:T(1024)S(1)}, f32[1024]{0:T(1024)}, u32[]{:S(2)}) copy-start(f32[1024]{0:T(1024)} %param.20) | copy-start | bytes 12292
  293.7 215.4 %all-gather.7.cloned.1.call-start = ((), (), s32[]{:S(2)}) async-start(), calls=%async_computation.6 | async-start | bytes 12582912 | tf_op jit(solution)/shard_map/all_gather | solution.py:364
  401.5 107.6 %copy-start.34 = (f32[2048]{0:T(1024)S(1)}, f32[2048]{0:T(1024)}, u32[]{:S(2)}) copy-start(f32[2048]{0:T(1024)} %param.22) | copy-start | bytes 24580
  405.0 209.6 %all-gather.9.cloned.1.call-start = ((), (), s32[]{:S(2)}) async-start(), calls=%async_computation.8 | async-start | bytes 12582912 | tf_op jit(solution)/shard_map/all_gather | solution.py:365
  405.6 377.5 %reduce-scatter.9.cloned.1.call-start = ((), (), s32[]{:S(2)}) async-start(), calls=%async_computation.9 | async-start | bytes 12582912 | tf_op jit(solution)/shard_map/reduce_scatter | solution.py:384
  683.5 99.5 %copy-start.9 = (f32[2048]{0:T(1024)S(1)}, f32[2048]{0:T(1024)}, u32[]{:S(2)}) copy-start(f32[2048]{0:T(1024)} %copy-done.8) | copy-start | bytes 24580
  683.5 99.5 %copy-start.14 = (f32[2048]{0:T(1024)S(1)}, f32[2048]{0:T(1024)}, u32[]{:S(2)}) copy-start(f32[2048]{0:T(1024)} %copy-done.13) | copy-start | bytes 24580
  683.5 99.5 %copy-start.23 = (f32[1024]{0:T(1024)S(1)}, f32[1024]{0:T(1024)}, u32[]{:S(2)}) copy-start(f32[1024]{0:T(1024)} %param.19) | copy-start | bytes 12292
  683.5 220.5 %all-gather.11.cloned.1.call-start = ((), (), s32[]{:S(2)}) async-start(), calls=%async_computation.10 | async-start | bytes 12582912 | tf_op jit(solution)/shard_map/all_gather | solution.py:394
  799.9 579.7 %all-reduce.4.cloned.1.call-start = ((), (), s32[]{:S(2)}) async-start(), calls=%async_computation.12 | async-start | bytes 25165824 | tf_op jit(solution)/shard_map/psum | solution.py:429
  1146.9 335.0 %reduce-scatter.11.cloned.1.call-start = ((), (), s32[]{:S(2)}) async-start(), calls=%async_computation.11 | async-start | bytes 12582912 | tf_op jit(solution)/shard_map/reduce_scatter | solution.py:415
  1165.5 418.7 %reduce-scatter.7.cloned.1.call-start = ((), (), s32[]{:S(2)}) async-start(), calls=%async_computation.7 | async-start | bytes 12582912 | tf_op jit(solution)/shard_map/reduce_scatter | solution.py:369
  1395.3 188.9 %copy-start.10 = (f32[2048]{0:T(1024)S(1)}, f32[2048]{0:T(1024)}, u32[]{:S(2)}) copy-start(f32[2048]{0:T(1024)} %copy-done.8) | copy-start | bytes 24580
  1395.3 188.9 %copy-start.15 = (f32[2048]{0:T(1024)S(1)}, f32[2048]{0:T(1024)}, u32[]{:S(2)}) copy-start(f32[2048]{0:T(1024)} %copy-done.13) | copy-start | bytes 24580
  1395.3 188.9 %copy-start.19 = (f32[2048]{0:T(1024)S(1)}, f32[2048]{0:T(1024)}, u32[]{:S(2)}) copy-start(f32[2048]{0:T(1024)} %copy-done.18) | copy-start | bytes 24580
  1395.3 188.9 %copy-start.21 = (f32[2048]{0:T(1024)S(1)}, f32[2048]{0:T(1024)}, u32[]{:S(2)}) copy-start(f32[2048]{0:T(1024)} %copy-done.20) | copy-start | bytes 24580
  1395.3 188.9 %copy-start.24 = (f32[1024]{0:T(1024)S(1)}, f32[1024]{0:T(1024)}, u32[]{:S(2)}) copy-start(f32[1024]{0:T(1024)} %param.19) | copy-start | bytes 12292
  1395.3 188.9 %copy-start.32 = (f32[1024]{0:T(1024)S(1)}, f32[1024]{0:T(1024)}, u32[]{:S(2)}) copy-start(f32[1024]{0:T(1024)} %param.24) | copy-start | bytes 12292
  1488.1 113.1 %copy-start.27 = (f32[1024]{0:T(1024)S(1)}, f32[1024]{0:T(1024)}, u32[]{:S(2)}) copy-start(f32[1024]{0:T(1024)} %get-tuple-element.40) | copy-start | bytes 12292
  1488.1 113.1 %copy-start.28 = (f32[1024]{0:T(1024)S(1)}, f32[1024]{0:T(1024)}, u32[]{:S(2)}) copy-start(f32[1024]{0:T(1024)} %get-tuple-element.46) | copy-start | bytes 12292
  (21 other events, 352.8 us)
Sparse Core Ops, SparseCore 0:
  17.1 106.6 all-gather.4
  293.8 99.3 reduce-scatter.4
  405.1 103.9 all-gather.6
  510.5 103.9 all-gather.8
  683.7 99.3 reduce-scatter.8
  800.1 103.9 all-gather.10
  1147.0 232.6 all-reduce.3
  1382.5 99.3 reduce-scatter.10
  1484.8 99.3 reduce-scatter.6
